TPU v7x, 256 devices: a whole 4x4x8 slice. The times are simulated.
256 devices in a mesh: high: 16 (over z, core), low: 16 (over y, x).
Axes of the slice: x: 4, y: 4, z: 8, core: 2. Of those that a mesh axis runs over, the one named last changes fastest.
Arguments:
- wave_parts: float32 [2, 1024, 128, 128], P(None, ('high', 'low')), may hold values from -6 to 6
- level_table: float32 [1024, 128, 128], P(('high', 'low')), may hold values from -2 to 2
- phase_angles: float32 [2, 128], replicated, may hold values from 0.3 to 1.2
- mix_angles: float32 [2, 4], replicated, may hold values from 0.3 to 1.2
Outputs:
- result_parts: float32 [2, 1024, 128, 128], P(None, ('high', 'low'))
- marginal: float32 [64, 128, 128], P('low', 'high')
All inputs are finite; a program needn't handle non-finite values.
Results may differ from a plain program's by a relative error of at most 0.0003.
Values sent between devices are 32-bit elements; how exact they have to be, the bound alone decides.
A program may use at most 64 MiB of HBM per device.

v0:
```python
import jax
import jax.numpy as jnp
from jax import lax
from jax.sharding import PartitionSpec as P

LAYERS = 2


def split_up(x, dim, size):
    lengths = x.shape
    blocks = x.reshape(*lengths[:dim], size, lengths[dim] // size, *lengths[dim + 1 :])
    return jnp.moveaxis(blocks, dim, 0)


def sent_and_summed(x, axis, dim):
    size = lax.axis_size(axis)
    blocks = lax.all_to_all(split_up(x, dim, size), axis, 0, 0, tiled=True)
    return jnp.sum(blocks, axis=0)


def count_bits(values, count):
    places = jnp.arange(count.bit_length() - 1, dtype=jnp.int32)
    return jnp.sum(values[..., None] >> places & 1, axis=-1)


def real_turn_table(count, angle):
    rank = jnp.arange(count, dtype=jnp.int32)
    apart = count_bits(rank[:, None] ^ rank[None, :], count)
    minus = count_bits(rank[:, None] & (rank[:, None] ^ rank[None, :]), count)
    bits = count.bit_length() - 1
    size = jnp.cos(angle) ** (bits - apart).astype(jnp.float32) * jnp.sin(angle) ** apart.astype(
        jnp.float32
    )
    return size * jnp.where(minus % 2 == 1, -1.0, 1.0).astype(jnp.float32)


def apply_along(values, dim, angle):
    real_part = real_turn_table(values.shape[dim], angle)
    moved = jnp.tensordot(values, real_part, axes=([dim], [0]), precision=lax.Precision.HIGHEST)
    return jnp.moveaxis(moved, -1, dim)


def phase_step(values, levels, angle):
    turn = angle * levels
    return jnp.stack(
        [
            values[0] * jnp.cos(turn) + values[1] * jnp.sin(turn),
            values[1] * jnp.cos(turn) - values[0] * jnp.sin(turn),
        ]
    )


def on_device(wave_parts, level_table, phase_angles, mix_angles):
    values = wave_parts
    for layer in range(LAYERS):
        values = phase_step(values, level_table, phase_angles[layer])
        values = apply_along(values, 3, mix_angles[layer, 0])
        values = apply_along(values, 2, mix_angles[layer, 1])
        moved = lax.all_to_all(values, "high", split_axis=2, concat_axis=1, tiled=True)
        moved = apply_along(moved, 1, mix_angles[layer, 2])
        values = lax.all_to_all(moved, "high", split_axis=1, concat_axis=2, tiled=True)
        moved = lax.all_to_all(values, "low", split_axis=3, concat_axis=1, tiled=True)
        spread = moved.reshape(2, lax.axis_size("low"), -1, moved.shape[2], moved.shape[3])
        moved = apply_along(spread, 1, mix_angles[layer, 3]).reshape(moved.shape)
        values = lax.all_to_all(moved, "low", split_axis=1, concat_axis=3, tiled=True)
    chance = values[0] * values[0] + values[1] * values[1]
    marginal = sent_and_summed(chance, "high", 1) / lax.axis_size("high")
    return (values, marginal)


def solution(mesh):
    in_specs = (P(None, ("high", "low"), None, None), P(("high", "low"), None, None), P(), P())
    out_specs = (P(None, ("high", "low"), None, None), P("low", "high", None))
    return jax.shard_map(
        on_device, mesh=mesh, in_specs=in_specs, out_specs=out_specs, check_vma=False
    )
```

profile of v0, /device:TPU:1, one launch (start us, length us, event | category | flops | bytes accessed | tf_op | source)
XLA Modules:
  0.0 197.7 jit_solution(17846921188193277231)
XLA Ops:
  0.6 1.7 fusion.158
  6.1 2.1 %fusion.14 = (f32[1,4,128,128]{3,2,1,0:T(8,128)S(1)}, f32[1,4,128,128]{3,2,1,0:T(8,128)S(1)}) fusion(f32[2,4,128,128]{3,2,1,0:T(8,128)} %param.4, f32[4,128,128]{2,1,0:T(8,128)} %param.5, f32[128]{0:T(128)S(1)} %get-tuple-element.25), kind=kLoop, calls=%fused_computation.31 | loop fusion | flops 458752 | bytes 1311232 | tf_op jit(solution)/shard_map/stack | solution.py:45
  8.1 0.8 fusion
  9.0 0.8 convolution_bitcast_fusion.5
  9.7 1.0 copy.95
  10.7 10.0 %all-to-all-start = ((f32[2,4,128,128]{3,1,0,2:T(4,128)}), f32[2,4,128,128]{3,1,0,2:T(4,128)S(1)}, u32[]{:S(2)}, u32[]{:S(2)}) async-start(f32[2,4,128,128]{3,1,0,2:T(4,128)} %copy.95), calls=%async_computation | async-start | bytes 1048576 | tf_op jit(solution)/shard_map/all_to_all | solution.py:59
  22.2 15.7 %all-to-all-done = f32[2,4,128,128]{3,1,0,2:T(4,128)S(1)} async-done(((f32[2,4,128,128]{3,1,0,2:T(4,128)}), f32[2,4,128,128]{3,1,0,2:T(4,128)S(1)}, u32[]{:S(2)}, u32[]{:S(2)}) %all-to-all-start) | async-done | bytes 524320 | tf_op jit(solution)/shard_map/all_to_all | solution.py:59
  39.4 20.0 %all_to_all.140 = f32[2,64,8,128]{3,2,0,1:T(8,128)S(1)} all-to-all(f32[2,64,8,128]{3,2,0,1:T(8,128)S(1)} %copy.99), channel_id=1, replica_groups=mesh['high'=16,'low'=16] {'high'}, dimensions={1} | all-to-all | bytes 1048576 | tf_op jit(solution)/shard_map/all_to_all | solution.py:61
  59.4 1.0 copy.102
  60.4 6.8 %all-to-all-start.2 = ((f32[2,4,128,128]{2,1,0,3:T(4,128)}), f32[2,4,128,128]{2,1,0,3:T(4,128)S(1)}, u32[]{:S(2)}, u32[]{:S(2)}) async-start(f32[2,4,128,128]{2,1,0,3:T(4,128)} %copy.102), calls=%async_computation.2 | async-start | bytes 1048576 | tf_op jit(solution)/shard_map/all_to_all | solution.py:62
  68.6 9.9 %all-to-all-done.2 = f32[2,4,128,128]{2,1,0,3:T(4,128)S(1)} async-done(((f32[2,4,128,128]{2,1,0,3:T(4,128)}), f32[2,4,128,128]{2,1,0,3:T(4,128)S(1)}, u32[]{:S(2)}, u32[]{:S(2)}) %all-to-all-start.2) | async-done | bytes 524320 | tf_op jit(solution)/shard_map/all_to_all | solution.py:62
  78.6 0.9 convolution_bitcast_fusion.3
  79.6 0.8 copy.107
  80.5 3.6 %all-to-all-start.3 = ((f32[2,64,128,8]{2,3,0,1:T(8,128)}), f32[2,64,128,8]{2,3,0,1:T(8,128)S(1)}, u32[]{:S(2)}, u32[]{:S(2)}) async-start(f32[2,64,128,8]{2,3,0,1:T(8,128)} %copy.107), calls=%async_computation.3 | async-start | bytes 1048576 | tf_op jit(solution)/shard_map/all_to_all | solution.py:65
  86.7 8.3 %all-to-all-done.3 = f32[2,64,128,8]{2,3,0,1:T(8,128)S(1)} async-done(((f32[2,64,128,8]{2,3,0,1:T(8,128)}), f32[2,64,128,8]{2,3,0,1:T(8,128)S(1)}, u32[]{:S(2)}, u32[]{:S(2)}) %all-to-all-start.3) | async-done | bytes 524320 | tf_op jit(solution)/shard_map/all_to_all | solution.py:65
  95.4 1.0 add_bitcast_fusion
  96.5 0.8 fusion.4
  97.3 0.8 convolution_bitcast_fusion.2
  98.1 1.0 copy.116
  99.1 4.8 %all-to-all-start.4 = ((f32[2,4,128,128]{3,1,0,2:T(4,128)}), f32[2,4,128,128]{3,1,0,2:T(4,128)S(1)}, u32[]{:S(2)}, u32[]{:S(2)}) async-start(f32[2,4,128,128]{3,1,0,2:T(4,128)} %copy.116), calls=%async_computation.4 | async-start | bytes 1048576 | tf_op jit(solution)/shard_map/all_to_all | solution.py:59
  105.5 15.8 %all-to-all-done.4 = f32[2,4,128,128]{3,1,0,2:T(4,128)S(1)} async-done(((f32[2,4,128,128]{3,1,0,2:T(4,128)}), f32[2,4,128,128]{3,1,0,2:T(4,128)S(1)}, u32[]{:S(2)}, u32[]{:S(2)}) %all-to-all-start.4) | async-done | bytes 524320 | tf_op jit(solution)/shard_map/all_to_all | solution.py:59
  122.7 19.9 %all_to_all.141 = f32[2,64,8,128]{3,2,0,1:T(8,128)S(1)} all-to-all(f32[2,64,8,128]{3,2,0,1:T(8,128)S(1)} %copy.120), channel_id=1, replica_groups=mesh['high'=16,'low'=16] {'high'}, dimensions={1} | all-to-all | bytes 1048576 | tf_op jit(solution)/shard_map/all_to_all | solution.py:61
  142.7 1.0 copy.123
  143.7 3.8 %all-to-all-start.6 = ((f32[2,4,128,128]{2,1,0,3:T(4,128)}), f32[2,4,128,128]{2,1,0,3:T(4,128)S(1)}, u32[]{:S(2)}, u32[]{:S(2)}) async-start(f32[2,4,128,128]{2,1,0,3:T(4,128)} %copy.123), calls=%async_computation.6 | async-start | bytes 1048576 | tf_op jit(solution)/shard_map/all_to_all | solution.py:62
  148.9 9.6 %all-to-all-done.6 = f32[2,4,128,128]{2,1,0,3:T(4,128)S(1)} async-done(((f32[2,4,128,128]{2,1,0,3:T(4,128)}), f32[2,4,128,128]{2,1,0,3:T(4,128)S(1)}, u32[]{:S(2)}, u32[]{:S(2)}) %all-to-all-start.6) | async-done | bytes 524320 | tf_op jit(solution)/shard_map/all_to_all | solution.py:62
  158.5 0.9 convolution_bitcast_fusion
  159.6 13.3 %all_to_all.142 = f32[2,64,128,8]{2,3,0,1:T(8,128)S(1)} all-to-all(f32[2,64,128,8]{2,3,0,1:T(8,128)S(1)} %copy.128), channel_id=1, replica_groups=mesh['high'=16,'low'=16] {'low'}, dimensions={1} | all-to-all | bytes 1048576 | tf_op jit(solution)/shard_map/all_to_all | solution.py:65
  173.0 2.8 %copy.131 = f32[1,4,128,16,8]{4,3,2,1,0:T(8,128)} copy(f32[1,4,128,16,8]{2,4,1,3,0:T(8,128)S(1)} %fusion.12) | data formatting | bytes 524288 | tf_op jit(solution)/shard_map/add | solution.py:66
  175.9 3.6 %add.47 = f32[4,16,8,128]{3,2,1,0:T(8,128)S(1)} reshape(f32[1,4,128,16,8]{4,3,2,1,0:T(8,128)} %copy.131) | data formatting | bytes 524288 | tf_op jit(solution)/shard_map/add | solution.py:66
  180.2 5.1 %all-to-all-start.8 = ((f32[16,4,8,128]{3,2,1,0:T(8,128)}), f32[16,4,8,128]{3,2,1,0:T(8,128)S(1)}, u32[]{:S(2)}, u32[]{:S(2)}) async-start(f32[16,4,8,128]{3,2,1,0:T(8,128)} %copy.132), calls=%async_computation.8 | async-start | bytes 524288 | tf_op jit(solution)/shard_map/all_to_all | solution.py:17
  185.4 1.0 copy.133
  186.4 10.7 %all-to-all-done.8 = f32[16,4,8,128]{3,2,1,0:T(8,128)S(1)} async-done(((f32[16,4,8,128]{3,2,1,0:T(8,128)}), f32[16,4,8,128]{3,2,1,0:T(8,128)S(1)}, u32[]{:S(2)}, u32[]{:S(2)}) %all-to-all-start.8) | async-done | bytes 262176 | tf_op jit(solution)/shard_map/all_to_all | solution.py:17
  (39 shorter events, 6.2 us)
Async XLA Ops:
  10.7 27.2 %all-to-all-start = ((f32[2,4,128,128]{3,1,0,2:T(4,128)}), f32[2,4,128,128]{3,1,0,2:T(4,128)S(1)}, u32[]{:S(2)}, u32[]{:S(2)}) async-start(f32[2,4,128,128]{3,1,0,2:T(4,128)} %copy.95), calls=%async_computation | async-start | bytes 1048576 | tf_op jit(solution)/shard_map/all_to_all | solution.py:59
  60.4 18.1 %all-to-all-start.2 = ((f32[2,4,128,128]{2,1,0,3:T(4,128)}), f32[2,4,128,128]{2,1,0,3:T(4,128)S(1)}, u32[]{:S(2)}, u32[]{:S(2)}) async-start(f32[2,4,128,128]{2,1,0,3:T(4,128)} %copy.102), calls=%async_computation.2 | async-start | bytes 1048576 | tf_op jit(solution)/shard_map/all_to_all | solution.py:62
  78.6 16.9 %copy-start = (f32[4,128,128]{2,1,0:T(8,128)S(1)}, f32[4,128,128]{2,1,0:T(8,128)}, u32[]{:S(2)}) copy-start(f32[4,128,128]{2,1,0:T(8,128)} %param.5) | copy-start | bytes 786436
  80.5 14.6 %all-to-all-start.3 = ((f32[2,64,128,8]{2,3,0,1:T(8,128)}), f32[2,64,128,8]{2,3,0,1:T(8,128)S(1)}, u32[]{:S(2)}, u32[]{:S(2)}) async-start(f32[2,64,128,8]{2,3,0,1:T(8,128)} %copy.107), calls=%async_computation.3 | async-start | bytes 1048576 | tf_op jit(solution)/shard_map/all_to_all | solution.py:65
  99.1 22.1 %all-to-all-start.4 = ((f32[2,4,128,128]{3,1,0,2:T(4,128)}), f32[2,4,128,128]{3,1,0,2:T(4,128)S(1)}, u32[]{:S(2)}, u32[]{:S(2)}) async-start(f32[2,4,128,128]{3,1,0,2:T(4,128)} %copy.116), calls=%async_computation.4 | async-start | bytes 1048576 | tf_op jit(solution)/shard_map/all_to_all | solution.py:59
  143.7 14.8 %all-to-all-start.6 = ((f32[2,4,128,128]{2,1,0,3:T(4,128)}), f32[2,4,128,128]{2,1,0,3:T(4,128)S(1)}, u32[]{:S(2)}, u32[]{:S(2)}) async-start(f32[2,4,128,128]{2,1,0,3:T(4,128)} %copy.123), calls=%async_computation.6 | async-start | bytes 1048576 | tf_op jit(solution)/shard_map/all_to_all | solution.py:62
  180.2 16.9 %all-to-all-start.8 = ((f32[16,4,8,128]{3,2,1,0:T(8,128)}), f32[16,4,8,128]{3,2,1,0:T(8,128)S(1)}, u32[]{:S(2)}, u32[]{:S(2)}) async-start(f32[16,4,8,128]{3,2,1,0:T(8,128)} %copy.132), calls=%async_computation.8 | async-start | bytes 524288 | tf_op jit(solution)/shard_map/all_to_all | solution.py:17
where the time goes:
time: 199 us; the launch traced here: 198 us
  waiting for transfers between devices  70.1 us (35%)
  blocking collectives  53.2 us (27%)
  starting transfers between devices  34 us (17%)
  local copies, waits for them, and re-layouts  17.8 us (9%)
  between operations  12.2 us (6%)
  matrix products  6.42 us (3%)
  other arithmetic  4 us (2%)
    all_to_all x2, blocking collectives, on_device(): lax.all_to_all(moved, 'high', split_axis=1, concat_axis=2, tiled=True)  39.9 us
    all_to_all x2, waiting for transfers between devices, on_device(): lax.all_to_all(values, 'high', split_axis=2, concat_axis=1, tiled=True)  31.5 us
    all_to_all x2, waiting for transfers between devices, on_device(): lax.all_to_all(values, 'low', split_axis=3, concat_axis=1, tiled=True)  19.5 us
    all_to_all x2, starting transfers between devices, on_device(): lax.all_to_all(values, 'high', split_axis=2, concat_axis=1, tiled=True)  14.8 us
    all_to_all x1, blocking collectives, on_device(): lax.all_to_all(moved, 'low', split_axis=1, concat_axis=3, tiled=True)  13.3 us
    all_to_all x1, waiting for transfers between devices, sent_and_summed(): blocks = lax.all_to_all(split_up(x, dim, size), axis, 0, 0, tiled=True)  10.7 us
    all_to_all x2, starting transfers between devices, on_device(): lax.all_to_all(values, 'low', split_axis=3, concat_axis=1, tiled=True)  10.5 us
    all_to_all x1, waiting for transfers between devices, on_device(): lax.all_to_all(moved, 'low', split_axis=1, concat_axis=3, tiled=True)  8.29 us
  transfers between devices with their start and end apart: 6, of which 6 were waited for; matrix products, arithmetic and copies ran while one was open for 1% of the time, Pallas kernels for 0%

commit v1 on v0

v1 whole, which is shorter than its diff:
```python
import functools

import jax
import jax.numpy as jnp
import numpy as np
from jax import lax
from jax.experimental import pallas as pl
from jax.experimental.pallas import tpu as pltpu
from jax.sharding import PartitionSpec as P

MESH = pl.DeviceIdType.MESH
T = 4
SUB, LANES = 8, 128
F32 = jnp.float32


def even_series(fn, terms, most):
    k = np.arange(4 * terms)
    y = (np.cos((k + 0.5) * np.pi / len(k)) + 1) / 2 * most**2
    basis = y[:, None] ** np.arange(terms)[None, :]
    return np.linalg.lstsq(basis, fn(np.sqrt(y)), rcond=None)[0]


COS = [float(c) for c in even_series(np.cos, 8, 2.5)]
SIN = [float(c) for c in even_series(lambda x: np.sin(x) / x, 8, 2.5)]


def cos_sin(x):
    y = x * x
    c, s = COS[-1], SIN[-1]
    for a, b in zip(COS[-2::-1], SIN[-2::-1]):
        c = c * y + a
        s = s * y + b
    return c, s * x


def turn_matrix(cos, sin, bits, left):
    size = 128 if bits is None else bits
    shape = (size, size)
    i = lax.broadcasted_iota(jnp.int32, shape, 1 if left else 0)
    j = lax.broadcasted_iota(jnp.int32, shape, 0 if left else 1)
    total = None
    for bit in range(len(cos)):
        a, b = (i >> bit) & 1, (j >> bit) & 1
        one = jnp.where(a == b, cos[bit], jnp.where(a > b, -sin[bit], sin[bit]))
        total = one if total is None else total * one
    return total


def butterflies(tiles, cos, sin):
    tiles = list(tiles)
    step = 1
    while step < len(tiles):
        for i in range(len(tiles)):
            if not i & step:
                u, v = tiles[i], tiles[i + step]
                tiles[i], tiles[i + step] = cos * u - sin * v, cos * v + sin * u
        step *= 2
    return tiles


def dot(a, b):
    return jnp.dot(a, b, precision=lax.Precision.HIGHEST, preferred_element_type=F32)


def kernel(
    n, wave, table, phase, mix, out, marg,
    s1, r1, s2, r2, m2, s3, r3, s4, r4, sq, rq, rt, rt2, cs, sn, mats,
    ssem, rsem, tssem, trsem,
):
    h, l = lax.axis_index("high"), lax.axis_index("low")
    half = n // 2

    def high(p):
        return (p, l)

    def low(q):
        return (h, q)

    barrier = pltpu.get_barrier_semaphore()

    def greet(d, _):
        pl.semaphore_signal(barrier, inc=1, device_id=high(lax.rem(h + d, n)), device_id_type=MESH)
        pl.semaphore_signal(barrier, inc=1, device_id=low(lax.rem(l + d, n)), device_id_type=MESH)
        return 0

    lax.fori_loop(1, n, greet, 0)

    def send_all(me, to, src_of, dst, send_sem, recv_sem):
        def one(p):
            pltpu.make_async_remote_copy(
                src_ref=src_of(p), dst_ref=dst, send_sem=send_sem, recv_sem=recv_sem,
                device_id=to(p), device_id_type=MESH,
            ).start()

        def both(d, _):
            one(lax.rem(me + d, n))
            one(lax.rem(me + n - d, n))
            return 0

        lax.fori_loop(1, half, both, 0)
        one(lax.rem(me + half, n))

    def waiter(ref, send_sem, recv_sem):
        return pltpu.make_async_remote_copy(
            src_ref=ref, dst_ref=ref, send_sem=send_sem, recv_sem=recv_sem,
            device_id=high(lax.rem(h + 1, n)), device_id_type=MESH,
        )

    mc, ms = cos_sin(mix[...])

    def of(layer, group):
        return mc[layer : layer + 1, group : group + 1], ms[layer : layer + 1, group : group + 1]

    row_bits = (n * SUB).bit_length() - 1
    lane_bits = LANES.bit_length() - 1
    c0, s0 = of(0, 1)
    mats[0, : n * SUB, : n * SUB] = turn_matrix([c0] * row_bits, [s0] * row_bits, n * SUB, True)
    c0, s0 = of(0, 0)
    mats[1] = turn_matrix([c0] * lane_bits, [s0] * lane_bits, LANES, False)
    c1, s1_ = of(1, 1)
    c2, s2_ = of(1, 2)
    mats[2, : n * SUB, : n * SUB] = turn_matrix(
        [c1] * 3 + [c2] * (row_bits - 3), [s1_] * 3 + [s2_] * (row_bits - 3), n * SUB, True
    )
    c1, s1_ = of(1, 0)
    mats[3] = turn_matrix([c1] * lane_bits, [s1_] * lane_bits, LANES, False)

    def wide(pair):
        return tuple(jnp.broadcast_to(x, (SUB, LANES)) for x in pair)

    pl.semaphore_wait(barrier, 2 * (n - 1))

    send_all(h, high, lambda p: table.at[:, p], rt.at[:, h], tssem.at[0], trsem.at[0])
    rt[:, pl.ds(h, 1)] = table[:, pl.ds(h, 1)]

    def first(t, _):
        angle = phase[0:1, :]
        co, si = cos_sin(table[t] * angle[None])
        re, im = wave[0, t], wave[1, t]
        for c, x in enumerate((re * co + im * si, im * co - re * si)):
            x = x.reshape(n * SUB, LANES)
            x = dot(dot(mats[0, : n * SUB, : n * SUB], x), mats[1])
            s1[t, :, c] = x.reshape(n, SUB, LANES)
        send_all(h, high, lambda p: s1.at[t, p], r1.at[t, h], ssem.at[0, t], rsem.at[0, t])
        r1[t, pl.ds(h, 1)] = s1[t, pl.ds(h, 1)]
        return 0

    lax.fori_loop(0, T, first, 0)

    waiter(rt.at[:, pl.ds(0, n - 1)], tssem.at[0], trsem.at[0]).wait_recv()
    send_all(l, low, lambda q: rt.at[:, q], rt2.at[:, l], tssem.at[1], trsem.at[1])
    rt2[:, pl.ds(l, 1)] = rt[:, pl.ds(l, 1)]

    hc, hs = wide(of(0, 2))

    def second(t, _):
        waiter(r1.at[t, pl.ds(0, n - 1)], ssem.at[0, t], rsem.at[0, t]).wait_recv()
        for c in range(2):
            tiles = butterflies([r1[t, i, c] for i in range(n)], hc, hs)
            for i in range(n):
                s2[t, i, c] = tiles[i]
        send_all(l, low, lambda q: s2.at[t, q], r2.at[t, l], ssem.at[1, t], rsem.at[1, t])
        r2[t, pl.ds(l, 1)] = s2[t, pl.ds(l, 1)]
        return 0

    lax.fori_loop(0, T, second, 0)

    waiter(rt2.at[:, pl.ds(0, n - 1)], tssem.at[1], trsem.at[1]).wait_recv()

    def factors(t, _):
        angle = phase[1:2, :]
        cs[t], sn[t] = cos_sin(rt2[t] * angle[None])
        return 0

    lax.fori_loop(0, T, factors, 0)

    lc, ls = wide(of(0, 3))

    def third(t, _):
        waiter(r2.at[t, pl.ds(0, n - 1)], ssem.at[1, t], rsem.at[1, t]).wait_recv()
        for c in range(2):
            tiles = butterflies([r2[t, i, c] for i in range(n)], lc, ls)
            for i in range(n):
                m2[t, i, c] = tiles[i]
        return 0

    lax.fori_loop(0, T, third, 0)

    tc2, ts2 = wide(of(1, 2))

    def middle(i, _):
        re = butterflies([m2[t, i, 0] for t in range(T)], hc, hs)
        im = butterflies([m2[t, i, 1] for t in range(T)], hc, hs)
        turned = ([], [])
        for t in range(T):
            co, si = cs[t, i], sn[t, i]
            turned[0].append(re[t] * co + im[t] * si)
            turned[1].append(im[t] * co - re[t] * si)
        for c in range(2):
            for t, x in enumerate(butterflies(turned[c], tc2, ts2)):
                m2[t, i, c] = x
        return 0

    lax.fori_loop(0, n, middle, 0)

    lc2, ls2 = wide(of(1, 3))

    def fourth(t, _):
        for c in range(2):
            tiles = butterflies([m2[t, i, c] for i in range(n)], lc2, ls2)
            for i in range(n):
                s3[t, i, c] = tiles[i]
        send_all(l, low, lambda q: s3.at[t, q], r3.at[t, l], ssem.at[2, t], rsem.at[2, t])
        r3[t, pl.ds(l, 1)] = s3[t, pl.ds(l, 1)]
        return 0

    lax.fori_loop(0, T, fourth, 0)

    def fifth(t, _):
        waiter(r3.at[t, pl.ds(0, n - 1)], ssem.at[2, t], rsem.at[2, t]).wait_recv()
        for c in range(2):
            x = r3[t, :, c].reshape(n * SUB, LANES)
            x = dot(dot(mats[2, : n * SUB, : n * SUB], x), mats[3])
            s4[t, :, c] = x.reshape(n, SUB, LANES)
        send_all(h, high, lambda p: s4.at[t, p], r4.at[t, h], ssem.at[3, t], rsem.at[3, t])
        r4[t, pl.ds(h, 1)] = s4[t, pl.ds(h, 1)]
        return 0

    lax.fori_loop(0, T, fifth, 0)

    rc, rs = wide(of(1, 1))

    def last(t, _):
        waiter(r4.at[t, pl.ds(0, n - 1)], ssem.at[3, t], rsem.at[3, t]).wait_recv()
        re = butterflies([r4[t, i, 0] for i in range(n)], rc, rs)
        im = butterflies([r4[t, i, 1] for i in range(n)], rc, rs)
        for i in range(n):
            out[0, t, i] = re[i]
            out[1, t, i] = im[i]
            sq[t, i] = re[i] * re[i] + im[i] * im[i]
        send_all(h, high, lambda p: sq.at[t, p], rq.at[t, h], ssem.at[4, t], rsem.at[4, t])
        rq[t, pl.ds(h, 1)] = sq[t, pl.ds(h, 1)]
        return 0

    lax.fori_loop(0, T, last, 0)

    def mean(t, _):
        waiter(rq.at[t, pl.ds(0, n - 1)], ssem.at[4, t], rsem.at[4, t]).wait_recv()
        total = rq[t, 0]
        for i in range(1, n):
            total = total + rq[t, i]
        marg[t] = total * (1.0 / n)
        return 0

    lax.fori_loop(0, T, mean, 0)

    def drain(t, _):
        for k, ref in enumerate((s1, s2, s3, s4, sq)):
            waiter(ref.at[t, pl.ds(0, n - 1)], ssem.at[k, t], rsem.at[k, t]).wait_send()
        return 0

    lax.fori_loop(0, T, drain, 0)
    waiter(rt.at[:, pl.ds(0, n - 1)], tssem.at[0], trsem.at[0]).wait_send()
    waiter(rt.at[:, pl.ds(0, n - 1)], tssem.at[1], trsem.at[1]).wait_send()


def on_device(n, wave_parts, level_table, phase_angles, mix_angles):
    wave = wave_parts.reshape(2, T, n, SUB, LANES)
    table = level_table.reshape(T, n, SUB, LANES)
    vmem = pl.BlockSpec(memory_space=pltpu.VMEM)
    state = pltpu.VMEM((T, n, 2, SUB, LANES), F32)
    half = pltpu.VMEM((T, n, SUB, LANES), F32)
    out, marg = pl.pallas_call(
        functools.partial(kernel, n),
        name="register",
        out_shape=(
            jax.ShapeDtypeStruct((2, T, n, SUB, LANES), F32),
            jax.ShapeDtypeStruct((T, SUB, LANES), F32),
        ),
        in_specs=[vmem] * 4,
        out_specs=(vmem, vmem),
        scratch_shapes=[state] * 9
        + [half] * 6
        + [
            pltpu.VMEM((4, LANES, LANES), F32),
            pltpu.SemaphoreType.DMA((5, T)),
            pltpu.SemaphoreType.DMA((5, T)),
            pltpu.SemaphoreType.DMA((2,)),
            pltpu.SemaphoreType.DMA((2,)),
        ],
        compiler_params=pltpu.CompilerParams(
            collective_id=0, has_side_effects=True, vmem_limit_bytes=24 * 1024 * 1024
        ),
    )(wave, table, phase_angles, mix_angles)
    return out.reshape(wave_parts.shape), marg


def solution(mesh):
    n = mesh.shape["high"]
    in_specs = (P(None, ("high", "low"), None, None), P(("high", "low"), None, None), P(), P())
    out_specs = (P(None, ("high", "low"), None, None), P("low", "high", None))
    return jax.shard_map(
        functools.partial(on_device, n), mesh=mesh, in_specs=in_specs, out_specs=out_specs, check_vma=False
    )
```

time: 199 us -> 67.4 us (0.34)
  waiting for transfers between devices: 70.1 us -> 0 us
  Pallas kernels: 0 us -> 62.5 us
  blocking collectives: 53.2 us -> 0 us
  starting transfers between devices: 34 us -> 0 us
  local copies, waits for them, and re-layouts: 17.8 us -> 4.07 us
  between operations: 12.2 us -> 0.66 us
  matrix products: 6.42 us -> 0 us
  other arithmetic: 4 us -> 0 us
    all_to_all x6 -> x0, waiting for transfers between devices: 70.1 us -> none  [the longest x2 31.5 us: on_device(): lax.all_to_all(values, 'high', split_axis=2, concat_axis=1, tiled=True)]
    pallas_call x0 -> x1, Pallas kernels: none -> 62.5 us  [on_device(): pl.pallas_call(functools.partial(kernel, n), name='register', out_shape=(...]
    all_to_all x3 -> x0, blocking collectives: 53.2 us -> none  [the longest x2 39.9 us: on_device(): lax.all_to_all(moved, 'high', split_axis=1, concat_axis=2, tiled=True)]
    all_to_all x6 -> x0, starting transfers between devices: 34 us -> none  [the longest x2 14.8 us: on_device(): lax.all_to_all(values, 'high', split_axis=2, concat_axis=1, tiled=True)]
    add x2 -> x0, local copies, waits for them, and re-layouts: 6.48 us -> none  [on_device(): chance = values[0] * values[0] + values[1] * values[1]]
    dot_general x8 -> x0, matrix products: 6.42 us -> none  [apply_along(): jnp.tensordot(values, real_part, axes=([dim], [0]), precision=lax.Precisi...]
    transpose x7 -> x0, local copies, waits for them, and re-layouts: 3.65 us -> none  [the longest x6 2.93 us: apply_along(): return jnp.moveaxis(moved, -1, dim)]
    another operation x2 -> x0, other arithmetic: 3.08 us -> none  [phase_step(): jnp.stack([values[0] * jnp.cos(turn) + values[1] * jnp.sin(turn), values[...]
  transfers between devices with their start and end apart: 6 -> 0, of which waited for: 6 -> 0; matrix products, arithmetic and copies ran while one was open for 1% -> 0% of each run, Pallas kernels for 0% -> 0%
where the time goes in v1:
time: 67.4 us; the launch traced here: 67.2 us
  Pallas kernels  62.5 us (93%)
  local copies, waits for them, and re-layouts  4.07 us (6%)
    pallas_call x1, Pallas kernels, on_device(): pl.pallas_call(functools.partial(kernel, n), name='register', out_shape=(...  62.5 us
    unnamed x10, local copies, waits for them, and re-layouts  4.07 us

profile of v1, /device:TPU:1, one launch (start us, length us, event | category | flops | bytes accessed | tf_op | source)
XLA Modules:
  0.0 67.2 jit_solution(15918027276419851093)
XLA Ops:
  0.6 0.0 copy-start.3
  0.6 0.0 copy-start.2
  0.7 0.7 copy-done.3
  1.3 0.0 copy-done.2
  1.3 0.0 copy-start
  1.3 1.0 %copy-done = f32[2,4,128,128]{3,2,1,0:T(8,128)S(1)} copy-done((f32[2,4,128,128]{3,2,1,0:T(8,128)S(1)}, f32[2,4,128,128]{3,2,1,0:T(8,128)}, u32[]{:S(2)}) %copy-start) | copy-done | bytes 524312
  2.4 0.0 copy-start.1
  2.4 0.9 %copy-done.1 = f32[4,128,128]{2,1,0:T(8,128)S(1)} copy-done((f32[4,128,128]{2,1,0:T(8,128)S(1)}, f32[4,128,128]{2,1,0:T(8,128)}, u32[]{:S(2)}) %copy-start.1) | copy-done | bytes 262168
  3.3 62.5 %register.1 = (f32[2,4,16,8,128]{4,3,2,1,0:T(8,128)S(1)}, f32[4,8,128]{2,1,0:T(8,128)S(1)}) custom-call(f32[2,4,16,8,128]{4,3,2,1,0:T(8,128)S(1)} %bitcast.3, f32[4,16,8,128]{3,2,1,0:T(8,128)S(1)} %bitcast.5, f32[2,128]{1,0:T(2,128)S(1)} %copy-done.2, f32[2,4]{1,0:T(2,128)S(1)} %copy-done.3), custom_call_target="tpu_custom_call" | custom-call | tf_op jit(solution)/shard_map/register/pallas_call | solution.py:274
  65.8 0.8 %copy.8 = f32[2,4,128,128]{3,2,1,0:T(8,128)} copy(f32[2,4,128,128]{3,2,1,0:T(8,128)S(1)} %bitcast.4) | data formatting | bytes 1048576
  66.6 0.6 copy.9
Async XLA Ops:
  0.6 0.7 %copy-start.3 = (f32[2,4]{1,0:T(2,128)S(1)}, f32[2,4]{1,0:T(2,128)}, u32[]{:S(2)}) copy-start(f32[2,4]{1,0:T(2,128)} %mix.1) | copy-start | bytes 100
  0.6 0.7 %copy-start.2 = (f32[2,128]{1,0:T(2,128)S(1)}, f32[2,128]{1,0:T(2,128)}, u32[]{:S(2)}) copy-start(f32[2,128]{1,0:T(2,128)} %phase.1) | copy-start | bytes 3076
  1.3 1.0 %copy-start = (f32[2,4,128,128]{3,2,1,0:T(8,128)S(1)}, f32[2,4,128,128]{3,2,1,0:T(8,128)}, u32[]{:S(2)}) copy-start(f32[2,4,128,128]{3,2,1,0:T(8,128)} %param.4) | copy-start | bytes 1572868
  2.4 0.9 %copy-start.1 = (f32[4,128,128]{2,1,0:T(8,128)S(1)}, f32[4,128,128]{2,1,0:T(8,128)}, u32[]{:S(2)}) copy-start(f32[4,128,128]{2,1,0:T(8,128)} %param.5) | copy-start | bytes 786436

commit v2 on v1

v2 whole, which is shorter than its diff:
```python
import functools

import jax
import jax.numpy as jnp
import numpy as np
from jax import lax
from jax.experimental import pallas as pl
from jax.experimental.pallas import tpu as pltpu
from jax.sharding import PartitionSpec as P

MESH = pl.DeviceIdType.MESH
T = 4
SUB, LANES = 8, 128
F32 = jnp.float32


def even_series(fn, terms, most):
    k = np.arange(4 * terms)
    y = (np.cos((k + 0.5) * np.pi / len(k)) + 1) / 2 * most**2
    basis = y[:, None] ** np.arange(terms)[None, :]
    return np.linalg.lstsq(basis, fn(np.sqrt(y)), rcond=None)[0]


COS = [float(c) for c in even_series(np.cos, 8, 2.5)]
SIN = [float(c) for c in even_series(lambda x: np.sin(x) / x, 8, 2.5)]


def cos_sin(x):
    y = x * x
    c, s = COS[-1], SIN[-1]
    for a, b in zip(COS[-2::-1], SIN[-2::-1]):
        c = c * y + a
        s = s * y + b
    return c, s * x


def turn_matrix(cos, sin, bits, left):
    size = 128 if bits is None else bits
    shape = (size, size)
    i = lax.broadcasted_iota(jnp.int32, shape, 1 if left else 0)
    j = lax.broadcasted_iota(jnp.int32, shape, 0 if left else 1)
    total = None
    for bit in range(len(cos)):
        a, b = (i >> bit) & 1, (j >> bit) & 1
        one = jnp.where(a == b, cos[bit], jnp.where(a > b, -sin[bit], sin[bit]))
        total = one if total is None else total * one
    return total


def butterflies(tiles, cos, sin):
    tiles = list(tiles)
    step = 1
    while step < len(tiles):
        for i in range(len(tiles)):
            if not i & step:
                u, v = tiles[i], tiles[i + step]
                tiles[i], tiles[i + step] = cos * u - sin * v, cos * v + sin * u
        step *= 2
    return tiles


def dot(a, b):
    return jnp.dot(a, b, precision=lax.Precision.HIGHEST, preferred_element_type=F32)


def kernel(
    n, wave_in, table_in, phase_in, mix_in, out, marg,
    wave, table, phase, mix, s1, r1, s2, r2, s3, r3, s4, r4, y, sq, rq, rt, cs, sn, mats,
    isem, ssem, rsem, tssem, trsem, qssem, qrsem,
):
    h, l = lax.axis_index("high"), lax.axis_index("low")
    rows = n * SUB

    def high(p):
        return (p, l)

    def low(q):
        return (h, q)

    loads = [
        pltpu.make_async_copy(src, dst, isem.at[k])
        for k, (src, dst) in enumerate(((mix_in, mix), (phase_in, phase), (wave_in, wave), (table_in, table)))
    ]
    for load in loads:
        load.start()

    barrier = pltpu.get_barrier_semaphore()

    def greet(device):
        pl.semaphore_signal(barrier, inc=1, device_id=device, device_id_type=MESH)

    def greet_all(d, _):
        greet(high(lax.rem(h + d, n)))
        greet(low(lax.rem(l + d, n)))
        greet((l, lax.rem(h + d, n)))
        return 0

    lax.fori_loop(1, n, greet_all, 0)

    @pl.when(h != l)
    def _():
        greet((l, h))

    def push(src, dst, device, send_sem, recv_sem):
        pltpu.make_async_remote_copy(
            src_ref=src, dst_ref=dst, send_sem=send_sem, recv_sem=recv_sem,
            device_id=device, device_id_type=MESH,
        ).start()

    def far_first(one):
        one(lax.rem(h + n // 2, n))

        def both(d, _):
            one(lax.rem(h + n // 2 + d, n))
            one(lax.rem(h + n + n // 2 - d, n))
            return 0

        lax.fori_loop(1, n // 2, both, 0)

    side = 4 if n == 16 else 2
    offsets = [(a, b) for a in range(side) for b in range(side) if a or b]
    offsets.sort(key=lambda o: -sum(min(x, side - x) for x in o))

    def send_high(t, src, dst, k):
        far_first(lambda p: push(src.at[t, p], dst.at[t, h], high(p), ssem.at[k, t], rsem.at[k, t]))
        dst[t, pl.ds(h, 1)] = src[t, pl.ds(h, 1)]

    def send_low(t, src, dst, k):
        for a, b in offsets:
            q = lax.rem(l // side + a, side) * side + lax.rem(lax.rem(l, side) + b, side)
            push(src.at[t, q], dst.at[t, l], low(q), ssem.at[k, t], rsem.at[k, t])
        dst[t, pl.ds(l, 1)] = src[t, pl.ds(l, 1)]

    def waiter(ref, send_sem, recv_sem):
        return pltpu.make_async_remote_copy(
            src_ref=ref, dst_ref=ref, send_sem=send_sem, recv_sem=recv_sem,
            device_id=high(lax.rem(h + 1, n)), device_id_type=MESH,
        )

    def arrived(t, dst, k):
        waiter(dst.at[t, pl.ds(0, n - 1)], ssem.at[k, t], rsem.at[k, t]).wait_recv()

    loads[0].wait()
    mc, ms = cos_sin(mix[...])

    def of(layer, group):
        return mc[layer : layer + 1, group : group + 1], ms[layer : layer + 1, group : group + 1]

    def wide(pair):
        return tuple(jnp.broadcast_to(x, (SUB, LANES)) for x in pair)

    def matrix(parts, size, left):
        return turn_matrix([p[0] for p in parts], [p[1] for p in parts], size, left)

    row_bits = rows.bit_length() - 1
    lane_bits = LANES.bit_length() - 1
    mats[0, :rows, :rows] = matrix([of(0, 1)] * row_bits, rows, True)
    mats[1] = matrix([of(0, 0)] * lane_bits, LANES, False)
    mats[2, :rows, :rows] = matrix([of(1, 1)] * 3 + [of(1, 2)] * (row_bits - 3), rows, True)
    mats[3] = matrix([of(1, 0)] * lane_bits, LANES, False)
    h1, l1 = wide(of(0, 2)), wide(of(0, 3))
    l2, r2w, t2 = wide(of(1, 3)), wide(of(1, 1)), wide(of(1, 2))

    def turn_sides(x, left, right):
        x = x.reshape(rows, LANES)
        return dot(dot(mats[left, :rows, :rows], x), mats[right]).reshape(n, SUB, LANES)

    for load in loads[1:]:
        load.wait()

    def first(i, _):
        parts = ([], [])
        for t in range(T):
            co, si = cos_sin(table[t, i] * phase[0:1, :])
            re, im = wave[0, t, i], wave[1, t, i]
            parts[0].append(re * co + im * si)
            parts[1].append(im * co - re * si)
        for c in range(2):
            for t, x in enumerate(butterflies(parts[c], *h1)):
                s1[t, i, c] = x
        return 0

    lax.fori_loop(0, n, first, 0)

    def rows_lanes(t):
        for c in range(2):
            s1[t, :, c] = turn_sides(s1[t, :, c], 0, 1)

    def send_table(t):
        def one(p):
            push(table.at[t, p], rt.at[t, l], (p, h), tssem.at[t], trsem.at[t])

        far_first(one)

        @pl.when(h != l)
        def _():
            one(h)

        @pl.when(h == l)
        def _():
            rt[t, pl.ds(l, 1)] = table[t, pl.ds(h, 1)]

    def turn_high(t):
        arrived(t, r1, 0)
        for c in range(2):
            tiles = butterflies([r1[t, i, c] for i in range(n)], *h1)
            for i in range(n):
                s2[t, i, c] = tiles[i]
        send_low(t, s2, r2, 1)

    def table_done(t, sent):
        @pl.when(h != l)
        def _():
            w = waiter(rt.at[t], tssem.at[t], trsem.at[t])
            w.wait_send() if sent else w.wait_recv()

        @pl.when(h == l)
        def _():
            w = waiter(rt.at[t, pl.ds(0, n - 1)], tssem.at[t], trsem.at[t])
            w.wait_send() if sent else w.wait_recv()

    def middle(t):
        table_done(t, False)

        def factors(i, _):
            co, si = cos_sin(rt[t, i] * phase[1:2, :])
            cs[t, i], sn[t, i] = co, si
            return 0

        lax.fori_loop(0, n, factors, 0)
        arrived(t, r2, 1)
        re = butterflies([r2[t, i, 0] for i in range(n)], *l1)
        im = butterflies([r2[t, i, 1] for i in range(n)], *l1)
        turned = ([], [])
        for i in range(n):
            co, si = cs[t, i], sn[t, i]
            turned[0].append(re[i] * co + im[i] * si)
            turned[1].append(im[i] * co - re[i] * si)
        for c in range(2):
            for i, x in enumerate(butterflies(turned[c], *l2)):
                s3[t, i, c] = x
        send_low(t, s3, r3, 2)

    def turn_back(t):
        arrived(t, r3, 2)
        for c in range(2):
            s4[t, :, c] = turn_sides(r3[t, :, c], 2, 3)
        send_high(t, s4, r4, 3)

    def turn_rows(t):
        arrived(t, r4, 3)
        for c in range(2):
            tiles = butterflies([r4[t, i, c] for i in range(n)], *r2w)
            for i in range(n):
                y[t, i, c] = tiles[i]

    rows_lanes(0)
    total = 3 * (n - 1)
    pl.semaphore_wait(barrier, jnp.where(h == l, total, total + 1))
    send_high(0, s1, r1, 0)
    for t in range(1, T):
        rows_lanes(t)
        send_high(t, s1, r1, 0)
        if t >= 1:
            send_table(t - 1)
    send_table(T - 1)

    turn_high(0)
    turn_high(1)
    middle(0)
    turn_high(2)
    middle(1)
    turn_back(0)
    turn_high(3)
    middle(2)
    turn_back(1)
    middle(3)
    turn_back(2)
    turn_back(3)
    for t in range(T):
        turn_rows(t)

    def finish(p):
        re = butterflies([y[t, p, 0] for t in range(T)], *t2)
        im = butterflies([y[t, p, 1] for t in range(T)], *t2)
        for t in range(T):
            out[0, t, pl.ds(p, 1)] = re[t][None]
            out[1, t, pl.ds(p, 1)] = im[t][None]
            sq[p, t] = re[t] * re[t] + im[t] * im[t]

    def share(p):
        finish(p)
        push(sq.at[p], rq.at[h], high(p), qssem, qrsem)

    far_first(share)
    finish(h)
    rq[pl.ds(h, 1)] = sq[pl.ds(h, 1)]
    waiter(rq.at[pl.ds(0, n - 1)], qssem, qrsem).wait_recv()
    for t in range(T):
        total = rq[0, t]
        for i in range(1, n):
            total = total + rq[i, t]
        marg[t] = total * (1.0 / n)

    for t in range(T):
        for k, ref in enumerate((s1, s2, s3, s4)):
            waiter(ref.at[t, pl.ds(0, n - 1)], ssem.at[k, t], rsem.at[k, t]).wait_send()
        table_done(t, True)
    waiter(sq.at[pl.ds(0, n - 1)], qssem, qrsem).wait_send()


def on_device(n, wave_parts, level_table, phase_angles, mix_angles):
    wave = wave_parts.reshape(2, T, n, SUB, LANES)
    table = level_table.reshape(T, n, SUB, LANES)
    vmem, hbm = pl.BlockSpec(memory_space=pltpu.VMEM), pl.BlockSpec(memory_space=pltpu.HBM)
    state = pltpu.VMEM((T, n, 2, SUB, LANES), F32)
    half = pltpu.VMEM((T, n, SUB, LANES), F32)
    share = pltpu.VMEM((n, T, SUB, LANES), F32)
    dma = pltpu.SemaphoreType.DMA
    out, marg = pl.pallas_call(
        functools.partial(kernel, n),
        name="register",
        out_shape=(
            jax.ShapeDtypeStruct((2, T, n, SUB, LANES), F32),
            jax.ShapeDtypeStruct((T, SUB, LANES), F32),
        ),
        in_specs=[hbm] * 4,
        out_specs=(vmem, vmem),
        scratch_shapes=[
            pltpu.VMEM(wave.shape, F32),
            half,
            pltpu.VMEM(phase_angles.shape, F32),
            pltpu.VMEM(mix_angles.shape, F32),
        ]
        + [state] * 9
        + [share] * 2
        + [half] * 3
        + [pltpu.VMEM((4, LANES, LANES), F32)]
        + [dma((4,)), dma((4, T)), dma((4, T)), dma((T,)), dma((T,)), dma, dma],
        compiler_params=pltpu.CompilerParams(
            collective_id=0, has_side_effects=True, vmem_limit_bytes=24 * 1024 * 1024
        ),
    )(*(pltpu.with_memory_space_constraint(x, pltpu.HBM) for x in (wave, table, phase_angles, mix_angles)))
    return out.reshape(wave_parts.shape), marg


def solution(mesh):
    n = mesh.shape["high"]
    in_specs = (P(None, ("high", "low"), None, None), P(("high", "low"), None, None), P(), P())
    out_specs = (P(None, ("high", "low"), None, None), P("low", "high", None))
    return jax.shard_map(
        functools.partial(on_device, n), mesh=mesh, in_specs=in_specs, out_specs=out_specs, check_vma=False
    )
```

time: 67.4 us -> 57.6 us (0.85)
  Pallas kernels: 62.5 us -> 55.5 us
  local copies, waits for them, and re-layouts: 4.07 us -> 1.4 us
    pallas_call x1, Pallas kernels: 62.5 us -> 55.5 us  [on_device(): pl.pallas_call(functools.partial(kernel, n), name='register', out_shape=(...]
    unnamed x10 -> x2, local copies, waits for them, and re-layouts: 4.07 us -> 1.4 us
where the time goes in v2:
time: 57.6 us; the launch traced here: 57.5 us
  Pallas kernels  55.5 us (96%)
  local copies, waits for them, and re-layouts  1.4 us (2%)
  between operations  0.64 us (1%)
    pallas_call x1, Pallas kernels, on_device(): pl.pallas_call(functools.partial(kernel, n), name='register', out_shape=(...  55.5 us
    unnamed x2, local copies, waits for them, and re-layouts  1.4 us

profile of v2, /device:TPU:1, one launch (start us, length us, event | category | flops | bytes accessed | tf_op | source)
XLA Modules:
  0.0 57.5 jit_solution(3477884753048825792)
XLA Ops:
  0.6 55.5 %register.1 = (f32[2,4,16,8,128]{4,3,2,1,0:T(8,128)S(1)}, f32[4,8,128]{2,1,0:T(8,128)S(1)}) custom-call(f32[2,4,16,8,128]{4,3,2,1,0:T(8,128)} %bitcast.4, f32[4,16,8,128]{3,2,1,0:T(8,128)} %bitcast.5, f32[2,128]{1,0:T(2,128)} %phase_in.1, f32[2,4]{1,0:T(2,128)} %mix_in.1), custom_call_target="tpu_custom_call" | custom-call | tf_op jit(solution)/shard_map/register/pallas_call | solution.py:320
  56.1 0.8 %copy.8 = f32[2,4,128,128]{3,2,1,0:T(8,128)} copy(f32[2,4,128,128]{3,2,1,0:T(8,128)S(1)} %bitcast.3) | data formatting | bytes 1048576
  56.9 0.6 %copy.9 = f32[4,8,128]{2,1,0:T(8,128)} copy(f32[4,8,128]{2,1,0:T(8,128)S(1)} %get-tuple-element.9) | data formatting | bytes 32768

commit v3 on v2

--- a/solution.py
+++ b/solution.py
@@ -59,14 +59,19 @@
     return tiles
 
 
+def split(x):
+    top = x.astype(jnp.bfloat16)
+    return top, (x - top.astype(F32)).astype(jnp.bfloat16)
+
+
 def dot(a, b):
-    return jnp.dot(a, b, precision=lax.Precision.HIGHEST, preferred_element_type=F32)
+    return sum(jnp.dot(x, y, preferred_element_type=F32) for x, y in ((a[0], b[0]), (a[0], b[1]), (a[1], b[0])))
 
 
 def kernel(
     n, wave_in, table_in, phase_in, mix_in, out, marg,
-    wave, table, phase, mix, s1, r1, s2, r2, s3, r3, s4, r4, y, sq, rq, rt, cs, sn, mats,
-    isem, ssem, rsem, tssem, trsem, qssem, qrsem,
+    wave, table, phase, mix, s1, r1, s2, r2, s3, r3, s4, r4, y, sq, pre, tot, rq, rt, cs, sn, mats,
+    ready, isem, ssem, rsem, tssem, trsem, pssem, prsem, qssem, qrsem,
 ):
     h, l = lax.axis_index("high"), lax.axis_index("low")
     rows = n * SUB
@@ -92,14 +97,9 @@
     def greet_all(d, _):
         greet(high(lax.rem(h + d, n)))
         greet(low(lax.rem(l + d, n)))
-        greet((l, lax.rem(h + d, n)))
         return 0
 
     lax.fori_loop(1, n, greet_all, 0)
-
-    @pl.when(h != l)
-    def _():
-        greet((l, h))
 
     def push(src, dst, device, send_sem, recv_sem):
         pltpu.make_async_remote_copy(
@@ -121,15 +121,15 @@
     offsets = [(a, b) for a in range(side) for b in range(side) if a or b]
     offsets.sort(key=lambda o: -sum(min(x, side - x) for x in o))
 
-    def send_high(t, src, dst, k):
-        far_first(lambda p: push(src.at[t, p], dst.at[t, h], high(p), ssem.at[k, t], rsem.at[k, t]))
-        dst[t, pl.ds(h, 1)] = src[t, pl.ds(h, 1)]
-
-    def send_low(t, src, dst, k):
+    def send_high(t, c, src, dst, k):
+        far_first(lambda p: push(src.at[t, c, p], dst.at[t, c, h], high(p), ssem.at[k, t, c], rsem.at[k, t, c]))
+        dst[t, c, pl.ds(h, 1)] = src[t, c, pl.ds(h, 1)]
+
+    def send_low(t, c, src, dst, k):
         for a, b in offsets:
             q = lax.rem(l // side + a, side) * side + lax.rem(lax.rem(l, side) + b, side)
-            push(src.at[t, q], dst.at[t, l], low(q), ssem.at[k, t], rsem.at[k, t])
-        dst[t, pl.ds(l, 1)] = src[t, pl.ds(l, 1)]
+            push(src.at[t, c, q], dst.at[t, c, l], low(q), ssem.at[k, t, c], rsem.at[k, t, c])
+        dst[t, c, pl.ds(l, 1)] = src[t, c, pl.ds(l, 1)]
 
     def waiter(ref, send_sem, recv_sem):
         return pltpu.make_async_remote_copy(
@@ -137,8 +137,8 @@
             device_id=high(lax.rem(h + 1, n)), device_id_type=MESH,
         )
 
-    def arrived(t, dst, k):
-        waiter(dst.at[t, pl.ds(0, n - 1)], ssem.at[k, t], rsem.at[k, t]).wait_recv()
+    def arrived(t, c, dst, k):
+        waiter(dst.at[t, c, pl.ds(0, n - 1)], ssem.at[k, t, c], rsem.at[k, t, c]).wait_recv()
 
     loads[0].wait()
     mc, ms = cos_sin(mix[...])
@@ -154,16 +154,22 @@
 
     row_bits = rows.bit_length() - 1
     lane_bits = LANES.bit_length() - 1
-    mats[0, :rows, :rows] = matrix([of(0, 1)] * row_bits, rows, True)
-    mats[1] = matrix([of(0, 0)] * lane_bits, LANES, False)
-    mats[2, :rows, :rows] = matrix([of(1, 1)] * 3 + [of(1, 2)] * (row_bits - 3), rows, True)
-    mats[3] = matrix([of(1, 0)] * lane_bits, LANES, False)
+    for k, made in enumerate(
+        (
+            matrix([of(0, 1)] * row_bits, rows, True),
+            matrix([of(0, 0)] * lane_bits, LANES, False),
+            matrix([of(1, 1)] * 3 + [of(1, 2)] * (row_bits - 3), rows, True),
+            matrix([of(1, 0)] * lane_bits, LANES, False),
+        )
+    ):
+        size = made.shape[0]
+        mats[k, 0, :size, :size], mats[k, 1, :size, :size] = split(made)
     h1, l1 = wide(of(0, 2)), wide(of(0, 3))
     l2, r2w, t2 = wide(of(1, 3)), wide(of(1, 1)), wide(of(1, 2))
 
     def turn_sides(x, left, right):
-        x = x.reshape(rows, LANES)
-        return dot(dot(mats[left, :rows, :rows], x), mats[right]).reshape(n, SUB, LANES)
+        x = dot((mats[left, 0, :rows, :rows], mats[left, 1, :rows, :rows]), split(x.reshape(rows, LANES)))
+        return dot(split(x), (mats[right, 0], mats[right, 1])).reshape(n, SUB, LANES)
 
     for load in loads[1:]:
         load.wait()
@@ -177,14 +183,14 @@
             parts[1].append(im * co - re * si)
         for c in range(2):
             for t, x in enumerate(butterflies(parts[c], *h1)):
-                s1[t, i, c] = x
+                s1[t, c, i] = x
         return 0
 
     lax.fori_loop(0, n, first, 0)
 
     def rows_lanes(t):
         for c in range(2):
-            s1[t, :, c] = turn_sides(s1[t, :, c], 0, 1)
+            s1[t, c] = turn_sides(s1[t, c], 0, 1)
 
     def send_table(t):
         def one(p):
@@ -201,12 +207,12 @@
             rt[t, pl.ds(l, 1)] = table[t, pl.ds(h, 1)]
 
     def turn_high(t):
-        arrived(t, r1, 0)
-        for c in range(2):
-            tiles = butterflies([r1[t, i, c] for i in range(n)], *h1)
+        for c in range(2):
+            arrived(t, c, r1, 0)
+            tiles = butterflies([r1[t, c, i] for i in range(n)], *h1)
             for i in range(n):
-                s2[t, i, c] = tiles[i]
-        send_low(t, s2, r2, 1)
+                s2[t, c, i] = tiles[i]
+            send_low(t, c, s2, r2, 1)
 
     def table_done(t, sent):
         @pl.when(h != l)
@@ -228,9 +234,10 @@
             return 0
 
         lax.fori_loop(0, n, factors, 0)
-        arrived(t, r2, 1)
-        re = butterflies([r2[t, i, 0] for i in range(n)], *l1)
-        im = butterflies([r2[t, i, 1] for i in range(n)], *l1)
+        arrived(t, 0, r2, 1)
+        re = butterflies([r2[t, 0, i] for i in range(n)], *l1)
+        arrived(t, 1, r2, 1)
+        im = butterflies([r2[t, 1, i] for i in range(n)], *l1)
         turned = ([], [])
         for i in range(n):
             co, si = cs[t, i], sn[t, i]
@@ -238,31 +245,39 @@
             turned[1].append(im[i] * co - re[i] * si)
         for c in range(2):
             for i, x in enumerate(butterflies(turned[c], *l2)):
-                s3[t, i, c] = x
-        send_low(t, s3, r3, 2)
+                s3[t, c, i] = x
+            send_low(t, c, s3, r3, 2)
 
     def turn_back(t):
-        arrived(t, r3, 2)
-        for c in range(2):
-            s4[t, :, c] = turn_sides(r3[t, :, c], 2, 3)
-        send_high(t, s4, r4, 3)
+        for c in range(2):
+            arrived(t, c, r3, 2)
+            s4[t, c] = turn_sides(r3[t, c], 2, 3)
+            send_high(t, c, s4, r4, 3)
 
     def turn_rows(t):
-        arrived(t, r4, 3)
-        for c in range(2):
-            tiles = butterflies([r4[t, i, c] for i in range(n)], *r2w)
+        for c in range(2):
+            arrived(t, c, r4, 3)
+            tiles = butterflies([r4[t, c, i] for i in range(n)], *r2w)
             for i in range(n):
-                y[t, i, c] = tiles[i]
+                y[t, c, i] = tiles[i]
 
     rows_lanes(0)
-    total = 3 * (n - 1)
-    pl.semaphore_wait(barrier, jnp.where(h == l, total, total + 1))
-    send_high(0, s1, r1, 0)
+    pl.semaphore_wait(barrier, 2 * (n - 1))
+    send_high(0, 0, s1, r1, 0)
+    send_high(0, 1, s1, r1, 0)
+
+    def tell(d, _):
+        pl.semaphore_signal(ready, inc=1, device_id=low(lax.rem(l + d, n)), device_id_type=MESH)
+        return 0
+
+    lax.fori_loop(1, n, tell, 0)
     for t in range(1, T):
         rows_lanes(t)
-        send_high(t, s1, r1, 0)
-        if t >= 1:
-            send_table(t - 1)
+        send_high(t, 0, s1, r1, 0)
+        send_high(t, 1, s1, r1, 0)
+        if t == 1:
+            pl.semaphore_wait(ready, n - 1)
+        send_table(t - 1)
     send_table(T - 1)
 
     turn_high(0)
@@ -281,41 +296,81 @@
         turn_rows(t)
 
     def finish(p):
-        re = butterflies([y[t, p, 0] for t in range(T)], *t2)
-        im = butterflies([y[t, p, 1] for t in range(T)], *t2)
+        re = butterflies([y[t, 0, p] for t in range(T)], *t2)
+        im = butterflies([y[t, 1, p] for t in range(T)], *t2)
         for t in range(T):
             out[0, t, pl.ds(p, 1)] = re[t][None]
             out[1, t, pl.ds(p, 1)] = im[t][None]
             sq[p, t] = re[t] * re[t] + im[t] * im[t]
 
-    def share(p):
+    chips = n // 2
+    z, core = h // 2, lax.rem(h, 2)
+
+    def chips_far_first(one):
+        one(lax.rem(z + chips // 2, chips))
+
+        def both(d, _):
+            one(lax.rem(z + chips // 2 + d, chips))
+            one(lax.rem(z + chips + chips // 2 - d, chips))
+            return 0
+
+        lax.fori_loop(1, chips // 2, both, 0)
+
+    def to_sibling(v):
+        p = 2 * v + 1 - core
         finish(p)
-        push(sq.at[p], rq.at[h], high(p), qssem, qrsem)
-
-    far_first(share)
-    finish(h)
-    rq[pl.ds(h, 1)] = sq[pl.ds(h, 1)]
-    waiter(rq.at[pl.ds(0, n - 1)], qssem, qrsem).wait_recv()
+        push(sq.at[p], pre.at[v], high(2 * z + 1 - core), pssem.at[v], prsem.at[v])
+        finish(2 * v + core)
+
+    def both_cores(v):
+        waiter(pre.at[v], pssem.at[v], prsem.at[v]).wait_recv()
+        tot[v] = sq[2 * v + core] + pre[v]
+
+    def to_chip(v):
+        both_cores(v)
+        push(tot.at[v], rq.at[z], high(2 * v + core), qssem, qrsem)
+
+    chips_far_first(to_sibling)
+    to_sibling(z)
+    chips_far_first(to_chip)
+    both_cores(z)
+    rq[pl.ds(z, 1)] = tot[pl.ds(z, 1)]
+    waiter(rq.at[pl.ds(0, chips - 1)], qssem, qrsem).wait_recv()
     for t in range(T):
         total = rq[0, t]
-        for i in range(1, n):
+        for i in range(1, chips):
             total = total + rq[i, t]
         marg[t] = total * (1.0 / n)
 
     for t in range(T):
         for k, ref in enumerate((s1, s2, s3, s4)):
-            waiter(ref.at[t, pl.ds(0, n - 1)], ssem.at[k, t], rsem.at[k, t]).wait_send()
+            for c in range(2):
+                waiter(ref.at[t, c, pl.ds(0, n - 1)], ssem.at[k, t, c], rsem.at[k, t, c]).wait_send()
         table_done(t, True)
-    waiter(sq.at[pl.ds(0, n - 1)], qssem, qrsem).wait_send()
+    for v in range(chips):
+        waiter(pre.at[v], pssem.at[v], prsem.at[v]).wait_send()
+    waiter(tot.at[pl.ds(0, chips - 1)], qssem, qrsem).wait_send()
+
+
+def put_out(state, marg, state_out, marg_out, sem):
+    copies = [
+        pltpu.make_async_copy(src, dst, sem.at[k]) for k, (src, dst) in enumerate(((state, state_out), (marg, marg_out)))
+    ]
+    for copy in copies:
+        copy.start()
+    for copy in copies:
+        copy.wait()
 
 
 def on_device(n, wave_parts, level_table, phase_angles, mix_angles):
     wave = wave_parts.reshape(2, T, n, SUB, LANES)
     table = level_table.reshape(T, n, SUB, LANES)
     vmem, hbm = pl.BlockSpec(memory_space=pltpu.VMEM), pl.BlockSpec(memory_space=pltpu.HBM)
-    state = pltpu.VMEM((T, n, 2, SUB, LANES), F32)
+    state = pltpu.VMEM((T, 2, n, SUB, LANES), F32)
     half = pltpu.VMEM((T, n, SUB, LANES), F32)
-    share = pltpu.VMEM((n, T, SUB, LANES), F32)
+    def share(count):
+        return pltpu.VMEM((count, T, SUB, LANES), F32)
+
     dma = pltpu.SemaphoreType.DMA
     out, marg = pl.pallas_call(
         functools.partial(kernel, n),
@@ -333,14 +388,25 @@
             pltpu.VMEM(mix_angles.shape, F32),
         ]
         + [state] * 9
-        + [share] * 2
+        + [share(n)]
+        + [share(n // 2)] * 3
         + [half] * 3
-        + [pltpu.VMEM((4, LANES, LANES), F32)]
-        + [dma((4,)), dma((4, T)), dma((4, T)), dma((T,)), dma((T,)), dma, dma],
+        + [pltpu.VMEM((4, 2, LANES, LANES), jnp.bfloat16)]
+        + [pltpu.SemaphoreType.REGULAR, dma((4,)), dma((4, T, 2)), dma((4, T, 2)), dma((T,)), dma((T,))]
+        + [dma((n // 2,)), dma((n // 2,)), dma, dma],
         compiler_params=pltpu.CompilerParams(
             collective_id=0, has_side_effects=True, vmem_limit_bytes=24 * 1024 * 1024
         ),
     )(*(pltpu.with_memory_space_constraint(x, pltpu.HBM) for x in (wave, table, phase_angles, mix_angles)))
+    out, marg = pl.pallas_call(
+        put_out,
+        name="put_out",
+        out_shape=(jax.ShapeDtypeStruct(out.shape, F32), jax.ShapeDtypeStruct(marg.shape, F32)),
+        in_specs=[vmem] * 2,
+        out_specs=(hbm, hbm),
+        scratch_shapes=[dma((2,))],
+        compiler_params=pltpu.CompilerParams(vmem_limit_bytes=8 * 1024 * 1024),
+    )(out, marg)
     return out.reshape(wave_parts.shape), marg
 
 

time: 57.6 us -> 54 us (0.938)
  Pallas kernels: 55.5 us -> 53.3 us
  local copies, waits for them, and re-layouts: 1.4 us -> 0 us
    pallas_call x1, Pallas kernels: 55.5 us -> 52.4 us  [on_device(): pl.pallas_call(functools.partial(kernel, n), name='register', out_shape=(...]
    unnamed x2 -> x0, local copies, waits for them, and re-layouts: 1.4 us -> none
    pallas_call x0 -> x1, Pallas kernels: none -> 0.81 us  [on_device(): pl.pallas_call(put_out, name='put_out', out_shape=(jax.ShapeDtypeStruct(o...]
where the time goes in v3:
time: 54 us; the launch traced here: 53.9 us
  Pallas kernels  53.3 us (99%)
  between operations  0.64 us (1%)
    pallas_call x1, Pallas kernels, on_device(): pl.pallas_call(functools.partial(kernel, n), name='register', out_shape=(...  52.4 us

profile of v3, /device:TPU:1, one launch (start us, length us, event | category | flops | bytes accessed | tf_op | source)
XLA Modules:
  0.0 53.9 jit_solution(13031849603439967466)
XLA Ops:
  0.6 52.4 %register.1 = (f32[2,4,16,8,128]{4,3,2,1,0:T(8,128)S(1)}, f32[4,8,128]{2,1,0:T(8,128)S(1)}) custom-call(f32[2,4,16,8,128]{4,3,2,1,0:T(8,128)} %bitcast.3, f32[4,16,8,128]{3,2,1,0:T(8,128)} %bitcast.4, f32[2,128]{1,0:T(2,128)} %phase_in.1, f32[2,4]{1,0:T(2,128)} %mix_in.1), custom_call_target="tpu_custom_call" | custom-call | tf_op jit(solution)/shard_map/register/pallas_call | solution.py:375
  53.1 0.8 %put_out.1 = (f32[2,4,16,8,128]{4,3,2,1,0:T(8,128)}, f32[4,8,128]{2,1,0:T(8,128)}) custom-call(f32[2,4,16,8,128]{4,3,2,1,0:T(8,128)S(1)} %get-tuple-element.6.state, f32[4,8,128]{2,1,0:T(8,128)S(1)} %get-tuple-element.7.marg), custom_call_target="tpu_custom_call" | custom-call | tf_op jit(solution)/shard_map/put_out/pallas_call | solution.py:401

commit v4 on v3

--- a/solution.py
+++ b/solution.py
@@ -271,14 +271,17 @@
         return 0
 
     lax.fori_loop(1, n, tell, 0)
-    for t in range(1, T):
-        rows_lanes(t)
-        send_high(t, 0, s1, r1, 0)
-        send_high(t, 1, s1, r1, 0)
-        if t == 1:
-            pl.semaphore_wait(ready, n - 1)
-        send_table(t - 1)
-    send_table(T - 1)
+    told = False
+    for what, t in [('T', 0), ('A', 1), ('T', 1), ('A', 2), ('T', 2), ('A', 3), ('T', 3)]:
+        if what == "A":
+            rows_lanes(t)
+            send_high(t, 0, s1, r1, 0)
+            send_high(t, 1, s1, r1, 0)
+        else:
+            if not told:
+                pl.semaphore_wait(ready, n - 1)
+                told = True
+            send_table(t)
 
     turn_high(0)
     turn_high(1)
@@ -307,14 +310,11 @@
     z, core = h // 2, lax.rem(h, 2)
 
     def chips_far_first(one):
-        one(lax.rem(z + chips // 2, chips))
-
-        def both(d, _):
-            one(lax.rem(z + chips // 2 + d, chips))
-            one(lax.rem(z + chips + chips // 2 - d, chips))
+        def each(d, _):
+            one(d + (d >= z).astype(jnp.int32))
             return 0
 
-        lax.fori_loop(1, chips // 2, both, 0)
+        lax.fori_loop(0, chips - 1, each, 0)
 
     def to_sibling(v):
         p = 2 * v + 1 - core

time: 54 us -> 52.4 us (0.970)
  Pallas kernels: 53.3 us -> 51.7 us
    pallas_call x1, Pallas kernels: 52.4 us -> 50.8 us  [on_device(): pl.pallas_call(functools.partial(kernel, n), name='register', out_shape=(...]
where the time goes in v4:
time: 52.4 us; the launch traced here: 52.3 us
  Pallas kernels  51.7 us (99%)
  between operations  0.64 us (1%)
    pallas_call x1, Pallas kernels, on_device(): pl.pallas_call(functools.partial(kernel, n), name='register', out_shape=(...  50.8 us

profile of v4, /device:TPU:1, one launch (start us, length us, event | category | flops | bytes accessed | tf_op | source)
XLA Modules:
  0.0 52.3 jit_solution(17254240063078124753)
XLA Ops:
  0.6 50.8 %register.1 = (f32[2,4,16,8,128]{4,3,2,1,0:T(8,128)S(1)}, f32[4,8,128]{2,1,0:T(8,128)S(1)}) custom-call(f32[2,4,16,8,128]{4,3,2,1,0:T(8,128)} %bitcast.3, f32[4,16,8,128]{3,2,1,0:T(8,128)} %bitcast.4, f32[2,128]{1,0:T(2,128)} %phase_in.1, f32[2,4]{1,0:T(2,128)} %mix_in.1), custom_call_target="tpu_custom_call" | custom-call | tf_op jit(solution)/shard_map/register/pallas_call | solution.py:375
  51.5 0.8 %put_out.1 = (f32[2,4,16,8,128]{4,3,2,1,0:T(8,128)}, f32[4,8,128]{2,1,0:T(8,128)}) custom-call(f32[2,4,16,8,128]{4,3,2,1,0:T(8,128)S(1)} %get-tuple-element.6.state, f32[4,8,128]{2,1,0:T(8,128)S(1)} %get-tuple-element.7.marg), custom_call_target="tpu_custom_call" | custom-call | tf_op jit(solution)/shard_map/put_out/pallas_call | solution.py:401

commit v5 on v4

--- a/solution.py
+++ b/solution.py
@@ -95,11 +95,12 @@
         pl.semaphore_signal(barrier, inc=1, device_id=device, device_id_type=MESH)
 
     def greet_all(d, _):
-        greet(high(lax.rem(h + d, n)))
-        greet(low(lax.rem(l + d, n)))
+        greet(high(lax.rem(h + n // 2 + d, n)))
+        greet(low(lax.rem(l + n // 2 + d, n)))
         return 0
 
-    lax.fori_loop(1, n, greet_all, 0)
+    lax.fori_loop(0, n // 2, greet_all, 0)
+    lax.fori_loop(n // 2 + 1, n, greet_all, 0)
 
     def push(src, dst, device, send_sem, recv_sem):
         pltpu.make_async_remote_copy(
@@ -121,13 +122,16 @@
     offsets = [(a, b) for a in range(side) for b in range(side) if a or b]
     offsets.sort(key=lambda o: -sum(min(x, side - x) for x in o))
 
+    down = [lax.rem(l // side + a, side) * side for a in range(side)]
+    along = [lax.rem(lax.rem(l, side) + b, side) for b in range(side)]
+    peers = [down[a] + along[b] for a, b in offsets]
+
     def send_high(t, c, src, dst, k):
         far_first(lambda p: push(src.at[t, c, p], dst.at[t, c, h], high(p), ssem.at[k, t, c], rsem.at[k, t, c]))
         dst[t, c, pl.ds(h, 1)] = src[t, c, pl.ds(h, 1)]
 
     def send_low(t, c, src, dst, k):
-        for a, b in offsets:
-            q = lax.rem(l // side + a, side) * side + lax.rem(lax.rem(l, side) + b, side)
+        for q in peers:
             push(src.at[t, c, q], dst.at[t, c, l], low(q), ssem.at[k, t, c], rsem.at[k, t, c])
         dst[t, c, pl.ds(l, 1)] = src[t, c, pl.ds(l, 1)]
 
@@ -335,12 +339,6 @@
     chips_far_first(to_chip)
     both_cores(z)
     rq[pl.ds(z, 1)] = tot[pl.ds(z, 1)]
-    waiter(rq.at[pl.ds(0, chips - 1)], qssem, qrsem).wait_recv()
-    for t in range(T):
-        total = rq[0, t]
-        for i in range(1, chips):
-            total = total + rq[i, t]
-        marg[t] = total * (1.0 / n)
 
     for t in range(T):
         for k, ref in enumerate((s1, s2, s3, s4)):
@@ -349,6 +347,14 @@
         table_done(t, True)
     for v in range(chips):
         waiter(pre.at[v], pssem.at[v], prsem.at[v]).wait_send()
+
+    waiter(rq.at[pl.ds(0, chips - 1)], qssem, qrsem).wait_recv()
+    for t in range(T):
+        total = rq[0, t]
+        for i in range(1, chips):
+            total = total + rq[i, t]
+        marg[t] = total * (1.0 / n)
+
     waiter(tot.at[pl.ds(0, chips - 1)], qssem, qrsem).wait_send()
 
 

time: 52.4 us -> 52.4 us (level)
  no operation moved by 1% of the time
where the time goes in v5:
time: 52.4 us; the launch traced here: 52.3 us
  Pallas kernels  51.6 us (98%)
  between operations  0.64 us (1%)
    pallas_call x1, Pallas kernels, on_device(): pl.pallas_call(functools.partial(kernel, n), name='register', out_shape=(...  50.8 us

profile of v5, /device:TPU:1, one launch (start us, length us, event | category | flops | bytes accessed | tf_op | source)
XLA Modules:
  0.0 52.3 jit_solution(8040075948850484004)
XLA Ops:
  0.6 50.8 %register.1 = (f32[2,4,16,8,128]{4,3,2,1,0:T(8,128)S(1)}, f32[4,8,128]{2,1,0:T(8,128)S(1)}) custom-call(f32[2,4,16,8,128]{4,3,2,1,0:T(8,128)} %bitcast.3, f32[4,16,8,128]{3,2,1,0:T(8,128)} %bitcast.4, f32[2,128]{1,0:T(2,128)} %phase_in.1, f32[2,4]{1,0:T(2,128)} %mix_in.1), custom_call_target="tpu_custom_call" | custom-call | tf_op jit(solution)/shard_map/register/pallas_call | solution.py:381
  51.4 0.8 %put_out.1 = (f32[2,4,16,8,128]{4,3,2,1,0:T(8,128)}, f32[4,8,128]{2,1,0:T(8,128)}) custom-call(f32[2,4,16,8,128]{4,3,2,1,0:T(8,128)S(1)} %get-tuple-element.6.state, f32[4,8,128]{2,1,0:T(8,128)S(1)} %get-tuple-element.7.marg), custom_call_target="tpu_custom_call" | custom-call | tf_op jit(solution)/shard_map/put_out/pallas_call | solution.py:407
